TPU v7x, 64 devices: a 2x2x8 block of a 4x4x8 slice. The times are simulated.
64 devices in a mesh: dp: 4 (over x, y), ep: 16 (over z, core).
Axes of the slice: x: 2, y: 2, z: 8, core: 2. Of those that a mesh axis runs over, the one named last changes fastest.
The devices are a block of a 4x4x8 slice.
Arguments:
- x: bfloat16 [32768, 4096], P(('dp', 'ep')), parts along dimension 0
- route_idx: int32 [32768, 2], P(('dp', 'ep')), parts along dimension 0
- gates: float32 [32768, 2], P(('dp', 'ep')), parts along dimension 0
- w1: bfloat16 [16, 4096, 1536], P('ep')
- w3: bfloat16 [16, 4096, 1536], P('ep')
- w2: bfloat16 [16, 1536, 4096], P('ep')
Outputs:
- output: bfloat16 [32768, 4096], P(('dp', 'ep')), parts along dimension 0
There are 4 independent parts. A program takes and returns all parts, laid end to end along the dimension named above; an argument that names none is the same for every part.
All inputs are finite; a program needn't handle non-finite values.
Results may differ from a plain program's by a relative error of at most 0.001.
Values are sent between devices in bfloat16 or wider.
A program may use at most 768 MiB of HBM per device.

v0:
```python
import jax
import jax.numpy as jnp
from jax import lax
from jax.sharding import PartitionSpec as P


def pair_slots(ne, e):
    n = e.shape[0]
    oh = (e[:, :, None] == jnp.arange(ne, dtype=e.dtype)).astype(jnp.float32)
    i = jnp.arange(n, dtype=jnp.int32)
    low = (i[None, :] < i[:, None]).astype(jnp.bfloat16)
    before = jnp.dot(low, jnp.sum(oh, axis=1).astype(jnp.bfloat16), preferred_element_type=jnp.float32)
    return jnp.sum(before[:, None, :] * oh, axis=2).astype(jnp.int32)


def dispatch(x, dest, nrows):
    r = jnp.arange(nrows, dtype=dest.dtype)[:, None]
    p = (dest[None, :, 0] == r) | (dest[None, :, 1] == r)
    return jnp.dot(p.astype(x.dtype), x)


def combine(back, dest, gates):
    r = jnp.arange(back.shape[0], dtype=dest.dtype)[None, :]
    o0 = jnp.dot((dest[:, 0:1] == r).astype(back.dtype), back, preferred_element_type=jnp.float32)
    o1 = jnp.dot((dest[:, 1:2] == r).astype(back.dtype), back, preferred_element_type=jnp.float32)
    return (gates[:, 0:1] * o0 + gates[:, 1:2] * o1).astype(jnp.bfloat16)


def expert_rows(rows, w1, w3, w2):
    a = jnp.dot(rows, w1, preferred_element_type=jnp.float32)
    b = jnp.dot(rows, w3, preferred_element_type=jnp.float32)
    h = (jax.nn.silu(a) * b).astype(jnp.bfloat16)
    return jnp.dot(h, w2, preferred_element_type=jnp.float32).astype(jnp.bfloat16)


def solution(mesh):
    ep = mesh.shape['ep']

    def local(x, route_idx, gates, w1, w3, w2):
        tok, d = x.shape
        cap = 3 * tok // 4
        dest = route_idx * cap + pair_slots(ep, route_idx)
        send = dispatch(x, dest, ep * cap).reshape(ep, cap, d)
        recv = lax.all_to_all(send, 'ep', 0, 0, tiled=True)
        out = lax.map(lambda rows: expert_rows(rows, w1[0], w3[0], w2[0]), recv)
        back = lax.all_to_all(out, 'ep', 0, 0, tiled=True)
        return combine(back.reshape(ep * cap, d), dest, gates)

    spec = P(('dp', 'ep'), None)
    wspec = P('ep', None, None)
    return jax.shard_map(local, mesh=mesh, in_specs=(spec, spec, spec, wspec, wspec, wspec),
                         out_specs=spec, check_vma=False)
```

profile of v0, /device:TPU:85, one launch (start us, length us, event | category | flops | bytes accessed | tf_op | source)
XLA Modules:
  0.0 2759.7 jit_solution(15949702133298315661)
XLA Ops:
  2.4 33.5 %fusion.39 = bf16[6144,4096]{1,0:T(8,128)(2,1)} fusion(bf16[512,4096]{1,0:T(8,128)(2,1)} %param.8, s32[512]{0:T(512)S(1)} %bitcast.60, s32[512]{0:T(512)S(1)} %bitcast.62), kind=kOutput, calls=%fused_computation.24 | convolution fusion | flops 25779240960 | bytes 54530048 | tf_op jit(solution)/shard_map/dot_general | solution.py:19
  35.9 9.1 all-to-all-start
  45.0 1082.2 %all-to-all-done = bf16[16,384,4096]{2,1,0:T(8,128)(2,1)} async-done(((bf16[16,384,4096]{2,1,0:T(8,128)(2,1)}), bf16[16,384,4096]{2,1,0:T(8,128)(2,1)}, u32[]{:S(2)}, u32[]{:S(2)}) %all-to-all-start) | async-done | bytes 50331680 | tf_op jit(solution)/shard_map/all_to_all | solution.py:44
  1127.3 475.3 %while.10 = (s32[]{:T(128)}, bf16[16,384,4096]{2,1,0:T(8,128)(2,1)}, bf16[16,384,4096]{2,1,0:T(8,128)(2,1)}, bf16[1,4096,1536]{2,1,0:T(8,128)(2,1)}, bf16[1,4096...) while((s32[]{:T(128)}, bf16[16,384,4096]{2,1,0:T(8,128)(2,1)}, ...), condition=%wide.region_3.4_spmd, body=%wide.region_2.3_spmd.sunk | while | flops 14500626432 | bytes 51906124 | solution.py:45
  1136.2 20.7 fusion.70
  1156.9 9.0 fusion.69
  1165.9 20.7 fusion.70
  1195.5 20.7 fusion.70
  1216.2 9.0 fusion.69
  1225.2 20.7 fusion.70
  1245.9 9.0 fusion.69
  1255.0 20.7 fusion.70
  1275.6 9.0 fusion.69
  1284.6 20.7 fusion.70
  1314.3 20.7 fusion.70
  1335.0 9.0 fusion.69
  1344.1 20.7 fusion.70
  1373.7 20.7 fusion.70
  1394.4 9.0 fusion.69
  1403.4 20.8 fusion.70
  1433.2 20.7 fusion.70
  1462.9 20.7 fusion.70
  1483.6 9.0 fusion.69
  1492.6 20.7 fusion.70
  1513.3 9.0 fusion.69
  1522.3 20.7 fusion.70
  1552.0 20.9 fusion.70
  1572.8 9.1 fusion.69
  1581.9 20.7 fusion.70
  1611.2 1082.7 %all-to-all-done.1 = bf16[16,384,4096]{2,1,0:T(8,128)(2,1)} async-done(((bf16[16,384,4096]{2,1,0:T(8,128)(2,1)}), bf16[16,384,4096]{2,1,0:T(8,128)(2,1)}, u32[]{:S(2)}, u32[]{:S(2)}) %all-to-all-start.1) | async-done | bytes 50331680 | tf_op jit(solution)/shard_map/all_to_all | solution.py:46
  2693.9 32.7 %fusion.37 = f32[512,4096]{1,0:T(8,128)} fusion(bf16[6144,4096]{1,0:T(8,128)(2,1)} %bitcast.9, s32[512]{0:T(512)S(1)} %bitcast.63), kind=kOutput, calls=%fused_computation.22 | convolution fusion | flops 25772949504 | bytes 58722304 | tf_op jit(solution)/shard_map/dot_general | solution.py:24
  2726.6 33.1 %add_convert_fusion = bf16[512,4096]{1,0:T(8,128)(2,1)} fusion(f32[512,4096]{1,0:T(8,128)} %fusion.37, bf16[6144,4096]{1,0:T(8,128)(2,1)} %bitcast.9, s32[512]{0:T(512)S(1)} %bitcast.61, f32[512]{0:T(512)S(1)} %bitcast.65, f32[512]{0:T(512)S(1)} %bitcast.64), kind=kOutput, calls=%fused_computation.26 | convolution fusion | flops 25781338112 | bytes 62920704 | tf_op jit(solution)/shard_map/dot_general | solution.py:25
  (25 shorter events, 73.6 us)
Async XLA Ops:
  2.4 33.5 %copy-start.1 = (s32[512,1]{0,1:T(1,128)}, s32[512,1]{0,1:T(1,128)S(1)}, u32[]{:S(2)}) copy-start(s32[512,1]{0,1:T(1,128)S(1)} %get-tuple-element.53) | copy-start | bytes 6148
  2.4 33.5 %copy-start.3 = (s32[512,1]{0,1:T(1,128)}, s32[512,1]{0,1:T(1,128)S(1)}, u32[]{:S(2)}) copy-start(s32[512,1]{0,1:T(1,128)S(1)} %get-tuple-element.52) | copy-start | bytes 6148
  35.9 1091.4 %all-to-all-start = ((bf16[16,384,4096]{2,1,0:T(8,128)(2,1)}), bf16[16,384,4096]{2,1,0:T(8,128)(2,1)}, u32[]{:S(2)}, u32[]{:S(2)}) async-start(bf16[16,384,4096]{2,1,0:T(8,128)(2,1)} %bitcast.59), calls=%async_computation | async-start | bytes 100663296 | tf_op jit(solution)/shard_map/all_to_all | solution.py:44
  1602.6 8.6 copy-start
  1602.6 1091.3 %copy-start.4 = (s32[512,1]{0,1:T(1,128)S(1)}, s32[512,1]{0,1:T(1,128)}, u32[]{:S(2)}) copy-start(s32[512,1]{0,1:T(1,128)} %copy-done.3) | copy-start | bytes 6148
  1602.6 1091.3 %all-to-all-start.1 = ((bf16[16,384,4096]{2,1,0:T(8,128)(2,1)}), bf16[16,384,4096]{2,1,0:T(8,128)(2,1)}, u32[]{:S(2)}, u32[]{:S(2)}) async-start(bf16[16,384,4096]{2,1,0:T(8,128)(2,1)} %get-tuple-element.37), calls=%async_computation.1 | async-start | bytes 100663296 | tf_op jit(solution)/shard_map/all_to_all | solution.py:46
  2693.9 32.7 %copy-start.2 = (s32[512,1]{0,1:T(1,128)S(1)}, s32[512,1]{0,1:T(1,128)}, u32[]{:S(2)}) copy-start(s32[512,1]{0,1:T(1,128)} %copy-done.1) | copy-start | bytes 6148
where the time goes:
time: 2760 us
  waiting for transfers between devices  2160 us (78%)
  matrix products  575 us (21%)
    all_to_all x1, waiting for transfers between devices, local(): back = lax.all_to_all(out, 'ep', 0, 0, tiled=True)  1080 us
    all_to_all x1, waiting for transfers between devices, local(): recv = lax.all_to_all(send, 'ep', 0, 0, tiled=True)  1080 us
    dot_general x16, matrix products, expert_rows(): jnp.dot(h, w2, preferred_element_type=jnp.float32).astype(jnp.bfloat16)  331 us
    dot_general x16, matrix products, expert_rows(): a = jnp.dot(rows, w1, preferred_element_type=jnp.float32)  144 us
  transfers between devices with their start and end apart: 2, of which 2 were waited for; matrix products, arithmetic and copies ran while one was open for 0% of the time, Pallas kernels for 0%

commit v1 on v0

v1 whole, which is shorter than its diff:
```python
import jax
import jax.numpy as jnp
from jax import lax
from jax.sharding import PartitionSpec as P

PARTS = (12, 18, 20, 14)


def weights(masks, g):
    m = masks.astype(jnp.float32)
    pair = jnp.sum(m, axis=(0, 3), keepdims=True) == 2.0
    w = jnp.sum(m * jnp.where(pair, g[None], 1.0), axis=3, keepdims=True)
    return jnp.where(jnp.sum(m, axis=3, keepdims=True) == 2.0, 1.0, w)


def merge(sources, cols):
    total = None
    for v, (w, empty) in zip(sources, cols):
        t = jnp.where(empty[:, None], 0.0, w[:, None] * v.astype(jnp.float32))
        total = t if total is None else total + t
    return total.astype(jnp.bfloat16)


def solution(mesh):
    ep = mesh.shape['ep']
    nz = ep // 2
    far = nz // 2

    def perm_z(step):
        return [(i, (i + 2 * step) % ep) for i in range(ep)]

    swap = [(i, i ^ 1) for i in range(ep)]

    def local(x, route_idx, gates, w1, w3, w2):
        tok, d = x.shape
        cuts = [tok * sum(PARTS[:k]) // sum(PARTS) for k in range(len(PARTS) + 1)]
        me = lax.axis_index('ep')
        z, c = me // 2, me % 2
        rr = lax.all_gather(jnp.concatenate([route_idx.astype(jnp.float32), gates], axis=1).T, 'ep')
        rr = lax.dynamic_index_in_dim(rr.reshape(nz, 2, 4, tok), c, 1, keepdims=False)
        home = (z + jnp.arange(nz)) % nz
        rr = jnp.take(rr, home, axis=0).transpose(0, 2, 1)
        re, rg = rr[..., :2].astype(jnp.int32), rr[..., 2:]

        def tables(sign):
            rel = (sign * (home[:, None, None] - re // 2)) % nz
            r = ((sign * jnp.arange(nz)) % nz)[:, None, None]
            inl = (rel > r) & (rel <= far) & (r <= far)
            ins = (rel > far) & ((r == 0) | ((r > far) & (rel < r)))
            return weights(jnp.stack([inl, ins, re == me, re == (me ^ 1)]), rg)

        tabs = {1: tables(1), -1: tables(-1)}
        outs = []
        xs = [lax.all_gather(x[lo:hi], 'ep') for lo, hi in zip(cuts, cuts[1:])]
        used = {j: (2, 3) if j == far else (0, 2, 3) if j < far else (1, 2, 3) for j in range(1, nz)}
        used[nz - far + 1] = (2, 3)
        used[0] = (0, 1, 2, 3)
        cols = {}
        for k in range(len(PARTS)):
            sign = 1 if k % 2 == 0 else -1
            for r, sources in used.items():
                for i in sources:
                    w = tabs[sign][i, (sign * r) % nz, cuts[k]:cuts[k + 1], 0]
                    cols[k, (sign * r) % nz, i] = w, w == 0.0
        xs[0], cols = lax.optimization_barrier((xs[0], cols))
        for k in range(len(PARTS)):
            sign = 1 if k % 2 == 0 else -1
            n = cuts[k + 1] - cuts[k]
            rows = xs[k].reshape(ep * n, d)
            a = jnp.dot(rows, w1[0], preferred_element_type=jnp.float32)
            b = jnp.dot(rows, w3[0], preferred_element_type=jnp.float32)
            h = (jax.nn.silu(a) * b).astype(jnp.bfloat16).reshape(nz, 2, n, -1)

            def out(core):
                part = lax.dynamic_index_in_dim(h, core, 1, keepdims=False).reshape(nz * n, -1)
                o = jnp.dot(part, w2[0], preferred_element_type=jnp.float32)
                return o.astype(jnp.bfloat16).reshape(nz, n, d)

            other = out(1 - c)
            par = lax.ppermute(other, 'ep', swap)
            own = out(c)

            def at(v, j):
                return lax.dynamic_index_in_dim(v, (z + j) % nz, 0, keepdims=False)

            def at_place(j, *sources):
                return [cols[k, j, i] for i in sources]

            def walk(first, step, source):
                msg = None
                for r in range(abs(first), 0, -1):
                    j = (r if first > 0 else -r) % nz
                    if msg is None:
                        msg = merge([at(own, j), at(par, j)], at_place(j, 2, 3))
                    else:
                        msg = merge([msg, at(own, j), at(par, j)], at_place(j, source, 2, 3))
                    msg = lax.ppermute(msg, 'ep', perm_z(step))
                return msg

            long = walk(sign * far, sign, 0)
            short = walk(-sign * (far - 1), -sign, 1)
            outs.append(merge([long, short, at(own, 0), at(par, 0)], at_place(0, 0, 1, 2, 3)))
        return jnp.concatenate(outs, axis=0)


    spec = P(('dp', 'ep'), None)
    wspec = P('ep', None, None)
    return jax.shard_map(local, mesh=mesh, in_specs=(spec, spec, spec, wspec, wspec, wspec),
                         out_specs=spec, check_vma=False)
```

time: 2760 us -> 888 us (0.32)
  waiting for transfers between devices: 2160 us -> 250 us
  matrix products: 575 us -> 417 us
  other arithmetic: 2.14 us -> 111 us
    all_to_all x2 -> x0, waiting for transfers between devices: 2160 us -> none  [the longest x1 1080 us: local(): back = lax.all_to_all(out, 'ep', 0, 0, tiled=True)]
    ppermute x0 -> x32, waiting for transfers between devices: none -> 192 us  [the longest x28 192 us: walk(): msg = lax.ppermute(msg, 'ep', perm_z(step))]
    dot_general x36 -> x16, matrix products: 575 us -> 417 us  [the longest x8 143 us: out(): o = jnp.dot(part, w2[0], preferred_element_type=jnp.float32)]
    convert_element_type x0 -> x21, other arithmetic: none -> 75.7 us  [the longest x20 75.7 us: merge(): return total.astype(jnp.bfloat16)]
    all_gather x0 -> x4, waiting for transfers between devices: none -> 58 us  [local(): xs = [lax.all_gather(x[lo:hi], 'ep') for lo, hi in zip(cuts, cuts[1:])]]
    ppermute x0 -> x32, starting transfers between devices: none -> 44 us  [the longest x28 41.9 us: walk(): msg = lax.ppermute(msg, 'ep', perm_z(step))]
    eq x0 -> x53, other arithmetic: none -> 32.2 us  [the longest x50 32.2 us: local(): cols[k, sign * r % nz, i] = (w, w == 0.0)]
  transfers between devices with their start and end apart: 2 -> 36, of which waited for: 2 -> 26; matrix products, arithmetic and copies ran while one was open for 0% -> 61% of each run, Pallas kernels for 0% -> 0%
where the time goes in v1:
time: 888 us; the launch traced here: 879 us
  matrix products  417 us (47%)
  waiting for transfers between devices  250 us (28%)
  other arithmetic  111 us (12%)
  starting transfers between devices  44.2 us (5%)
  local copies, waits for them, and re-layouts  20.2 us (2%)
  blocking collectives  20 us (2%)
  between operations  16.7 us (2%)
    ppermute x28, waiting for transfers between devices, walk(): msg = lax.ppermute(msg, 'ep', perm_z(step))  192 us
    dot_general x8, matrix products, out(): o = jnp.dot(part, w2[0], preferred_element_type=jnp.float32)  143 us
    dot_general x4, matrix products, local(): a = jnp.dot(rows, w1[0], preferred_element_type=jnp.float32)  138 us
    dot_general x4, matrix products, local(): b = jnp.dot(rows, w3[0], preferred_element_type=jnp.float32)  136 us
    convert_element_type x20, other arithmetic, merge(): return total.astype(jnp.bfloat16)  75.7 us
    all_gather x4, waiting for transfers between devices, local(): xs = [lax.all_gather(x[lo:hi], 'ep') for lo, hi in zip(cuts, cuts[1:])]  58 us
    ppermute x28, starting transfers between devices, walk(): msg = lax.ppermute(msg, 'ep', perm_z(step))  41.9 us
    eq x50, other arithmetic, local(): cols[k, sign * r % nz, i] = (w, w == 0.0)  32.2 us
  transfers between devices with their start and end apart: 36, of which 26 were waited for; matrix products, arithmetic and copies ran while one was open for 61% of the time, Pallas kernels for 0%

profile of v1, /device:TPU:85, one launch (start us, length us, event | category | flops | bytes accessed | tf_op | source)
XLA Modules:
  0.0 879.1 jit_solution(1220671978315630185)
XLA Ops:
  16.4 20.0 %all-gather.5 = f32[16,4,512]{2,1,0:T(4,128)S(1)} all-gather(f32[1,4,512]{2,1,0:T(4,128)S(1)} %maximum_bitcast_fusion), channel_id=3, replica_groups=mesh['dp'=4,'ep'=16] {'ep'}, dimensions={0}, use_global_device_ids=true | all-gather | bytes 139264 | tf_op jit(solution)/shard_map/all_gather | solution.py:39
  74.2 9.0 %all-gather.11.cloned.1.call-done = bf16[1536,4096]{1,0:T(8,128)(2,1)} async-done(((bf16[96,4096]{1,0:T(8,128)(2,1)}), bf16[1536,4096]{1,0:T(8,128)(2,1)}) %all-gather.11.cloned.1.call-update) | async-done | bytes 12582928 | tf_op jit(solution)/shard_map/all_gather | solution.py:54
  83.3 28.0 %fusion.24 = f32[1536,1536]{1,0:T(8,128)} fusion(bf16[1536,4096]{1,0:T(8,128)(2,1)} %all-gather.11.cloned.1.call-done, bf16[1,4096,1536]{2,1,0:T(8,128)(2,1)} %param.9), kind=kOutput, calls=%fused_computation.31 | convolution fusion | flops 19327352832 | bytes 34603008 | tf_op jit(solution)/shard_map/dot_general | solution.py:70
  111.7 27.2 %fusion.34 = bf16[1536,1536]{1,0:T(8,128)(2,1)S(1)} fusion(bf16[1536,4096]{1,0:T(8,128)(2,1)} %all-gather.11.cloned.1.call-done, bf16[1,4096,1536]{2,1,0:T(8,128)(2,1)} %param.10, f32[1536,1536]{1,0:T(8,128)} %fusion.24), kind=kOutput, calls=%fused_computation.36 | convolution fusion | flops 19341508608 | bytes 39321600 | tf_op jit(solution)/shard_map/dot_general | solution.py:71
  139.3 11.7 %fusion.46 = bf16[768,4096]{1,0:T(8,128)(2,1)} fusion(bf16[768,1536]{1,0:T(8,128)(2,1)S(1)} %bitcast.571, bf16[1,1536,4096]{2,1,0:T(8,128)(2,1)S(1)} %bitcast.652), kind=kOutput, calls=%fused_computation.40 | convolution fusion | flops 9666822144 | bytes 21233664 | tf_op jit(solution)/shard_map/dot_general | solution.py:76
  151.2 12.5 %fusion.43 = bf16[768,4096]{1,0:T(8,128)(2,1)} fusion(bf16[768,1536]{1,0:T(8,128)(2,1)S(1)} %bitcast.570, bf16[1,1536,4096]{2,1,0:T(8,128)(2,1)S(1)} %bitcast.652), kind=kOutput, calls=%fused_computation.39 | convolution fusion | flops 9666822144 | bytes 21233664 | tf_op jit(solution)/shard_map/dot_general | solution.py:76
  165.9 30.8 %fusion.18 = f32[1792,1536]{1,0:T(8,128)} fusion(bf16[1792,4096]{1,0:T(8,128)(2,1)} %all-gather.17.cloned.1.call-done, bf16[1,4096,1536]{2,1,0:T(8,128)(2,1)} %param.9), kind=kOutput, calls=%fused_computation.25 | convolution fusion | flops 22548578304 | bytes 38273024 | tf_op jit(solution)/shard_map/dot_general | solution.py:70
  200.9 30.8 %multiply_convert_fusion.1 = bf16[1792,1536]{1,0:T(8,128)(2,1)S(1)} fusion(f32[1792,1536]{1,0:T(8,128)} %fusion.18, bf16[1792,4096]{1,0:T(8,128)(2,1)} %all-gather.17.cloned.1.call-done, bf16[1,4096,1536]{2,1,0:T(8,128)(2,1)} %param.10), kind=kOutput, calls=%fused_computation.34 | convolution fusion | flops 22565093376 | bytes 43778048 | tf_op jit(solution)/shard_map/dot_general | solution.py:71
  240.9 16.7 %fusion.40 = bf16[896,4096]{1,0:T(8,128)(2,1)} fusion(bf16[896,1536]{1,0:T(8,128)(2,1)S(1)} %bitcast.569, bf16[1,1536,4096]{2,1,0:T(8,128)(2,1)} %param.11), kind=kOutput, calls=%fused_computation.38 | convolution fusion | flops 11277959168 | bytes 22675456 | tf_op jit(solution)/shard_map/dot_general | solution.py:76
  258.9 15.8 %collective-permute-done.2 = bf16[96,4096]{1,0:T(8,128)(2,1)S(1)} collective-permute-done((bf16[96,4096]{1,0:T(8,128)(2,1)S(1)}, bf16[96,4096]{1,0:T(8,128)(2,1)S(1)}, u32[]{:S(2)}, u32[]{:S(2)}) %collective-permute-start.2) | collective-permute-done | bytes 786464 | tf_op jit(solution)/shard_map/ppermute | solution.py:97
  283.9 31.3 %all-gather.13.cloned.1.call-done = bf16[2304,4096]{1,0:T(8,128)(2,1)} async-done(((bf16[144,4096]{1,0:T(8,128)(2,1)}), bf16[2304,4096]{1,0:T(8,128)(2,1)}) %all-gather.13.cloned.1.call-update) | async-done | bytes 18874384 | tf_op jit(solution)/shard_map/all_gather | solution.py:54
  315.2 37.6 %fusion.22 = f32[2304,1536]{1,0:T(8,128)} fusion(bf16[2304,4096]{1,0:T(8,128)(2,1)} %all-gather.13.cloned.1.call-done, bf16[1,4096,1536]{2,1,0:T(8,128)(2,1)} %param.9), kind=kOutput, calls=%fused_computation.29 | convolution fusion | flops 28991029248 | bytes 45613056 | tf_op jit(solution)/shard_map/dot_general | solution.py:70
  352.8 37.8 %fusion.26 = bf16[2304,1536]{1,0:T(8,128)(2,1)S(1)} fusion(bf16[2304,4096]{1,0:T(8,128)(2,1)} %all-gather.13.cloned.1.call-done, bf16[1,4096,1536]{2,1,0:T(8,128)(2,1)} %param.10, f32[2304,1536]{1,0:T(8,128)} %fusion.22), kind=kOutput, calls=%fused_computation.33 | convolution fusion | flops 29012262912 | bytes 52690944 | tf_op jit(solution)/shard_map/dot_general | solution.py:71
  393.0 20.6 %convolution_convert_fusion.2 = bf16[1152,4096]{1,0:T(8,128)(2,1)} fusion(bf16[1152,1536]{1,0:T(8,128)(2,1)S(1)} %bitcast.567, bf16[1,1536,4096]{2,1,0:T(8,128)(2,1)} %param.11), kind=kOutput, calls=%fused_computation.5 | convolution fusion | flops 14500233216 | bytes 25559040 | tf_op jit(solution)/shard_map/dot_general | solution.py:76
  413.9 15.6 %all-gather.15.cloned.1.call-done = bf16[2560,4096]{1,0:T(8,128)(2,1)} async-done(((bf16[160,4096]{1,0:T(8,128)(2,1)}), bf16[2560,4096]{1,0:T(8,128)(2,1)}) %all-gather.15.cloned.1.call-update) | async-done | bytes 20971536 | tf_op jit(solution)/shard_map/all_gather | solution.py:54
  429.4 41.1 %fusion.20 = f32[2560,1536]{1,0:T(8,128)} fusion(bf16[2560,4096]{1,0:T(8,128)(2,1)} %all-gather.15.cloned.1.call-done, bf16[1,4096,1536]{2,1,0:T(8,128)(2,1)} %param.9), kind=kOutput, calls=%fused_computation.27 | convolution fusion | flops 32212254720 | bytes 49283072 | tf_op jit(solution)/shard_map/dot_general | solution.py:70
  470.5 40.6 %multiply_convert_fusion = bf16[2560,1536]{1,0:T(8,128)(2,1)S(1)} fusion(f32[2560,1536]{1,0:T(8,128)} %fusion.20, bf16[2560,4096]{1,0:T(8,128)(2,1)} %all-gather.15.cloned.1.call-done, bf16[1,4096,1536]{2,1,0:T(8,128)(2,1)} %param.10), kind=kOutput, calls=%fused_computation.1 | convolution fusion | flops 32235847680 | bytes 57147392 | tf_op jit(solution)/shard_map/dot_general | solution.py:71
  512.0 22.4 %convolution_convert_fusion = bf16[1280,4096]{1,0:T(8,128)(2,1)} fusion(bf16[1280,1536]{1,0:T(8,128)(2,1)S(1)} %bitcast.565, bf16[1,1536,4096]{2,1,0:T(8,128)(2,1)} %param.11), kind=kOutput, calls=%fused_computation.3 | convolution fusion | flops 16111370240 | bytes 27000832 | tf_op jit(solution)/shard_map/dot_general | solution.py:76
  542.4 15.3 %fusion.37 = bf16[896,4096]{1,0:T(8,128)(2,1)S(1)} fusion(bf16[896,1536]{1,0:T(8,128)(2,1)} %bitcast.568, bf16[1,1536,4096]{2,1,0:T(8,128)(2,1)} %param.11), kind=kOutput, calls=%fused_computation.37 | convolution fusion | flops 11277959168 | bytes 22675456 | tf_op jit(solution)/shard_map/dot_general | solution.py:76
  567.1 21.5 %convolution_convert_fusion.3 = bf16[1152,4096]{1,0:T(8,128)(2,1)} fusion(bf16[1152,1536]{1,0:T(8,128)(2,1)} %bitcast.566, bf16[1,1536,4096]{2,1,0:T(8,128)(2,1)} %param.11), kind=kOutput, calls=%fused_computation.6 | convolution fusion | flops 14500233216 | bytes 25559040 | tf_op jit(solution)/shard_map/dot_general | solution.py:76
  588.7 22.2 %convolution_convert_fusion.1 = bf16[1280,4096]{1,0:T(8,128)(2,1)} fusion(bf16[1280,1536]{1,0:T(8,128)(2,1)S(1)} %bitcast.564, bf16[1,1536,4096]{2,1,0:T(8,128)(2,1)} %param.11), kind=kOutput, calls=%fused_computation.4 | convolution fusion | flops 16111370240 | bytes 27000832 | tf_op jit(solution)/shard_map/dot_general | solution.py:76
  626.0 14.9 %collective-permute-done.9 = bf16[144,4096]{1,0:T(8,128)(2,1)S(1)} collective-permute-done((bf16[144,4096]{1,0:T(8,128)(2,1)S(1)}, bf16[144,4096]{1,0:T(8,128)(2,1)S(1)}, u32[]{:S(2)}, u32[]{:S(2)}) %collective-permute-start.9) | collective-permute-done | bytes 1179680 | tf_op jit(solution)/shard_map/ppermute | solution.py:97
  654.6 6.0 collective-permute-done.26
  662.1 5.7 collective-permute-done.29
  673.5 12.4 %collective-permute-done.10 = bf16[144,4096]{1,0:T(8,128)(2,1)S(1)} collective-permute-done((bf16[144,4096]{1,0:T(8,128)(2,1)S(1)}, bf16[144,4096]{1,0:T(8,128)(2,1)S(1)}, u32[]{:S(2)}, u32[]{:S(2)}) %collective-permute-start.10) | collective-permute-done | bytes 1179680 | tf_op jit(solution)/shard_map/ppermute | solution.py:97
  699.2 21.9 %collective-permute-done.18 = bf16[160,4096]{1,0:T(8,128)(2,1)S(1)} collective-permute-done((bf16[160,4096]{1,0:T(8,128)(2,1)S(1)}, bf16[160,4096]{1,0:T(8,128)(2,1)S(1)}, u32[]{:S(2)}, u32[]{:S(2)}) %collective-permute-start.18) | collective-permute-done | bytes 1310752 | tf_op jit(solution)/shard_map/ppermute | solution.py:97
  735.1 5.7 collective-permute-done.30
  747.0 11.9 %collective-permute-done.11 = bf16[144,4096]{1,0:T(8,128)(2,1)S(1)} collective-permute-done((bf16[144,4096]{1,0:T(8,128)(2,1)S(1)}, bf16[144,4096]{1,0:T(8,128)(2,1)S(1)}, u32[]{:S(2)}, u32[]{:S(2)}) %collective-permute-start.11) | collective-permute-done | bytes 1179680 | tf_op jit(solution)/shard_map/ppermute | solution.py:97
  772.2 22.0 %collective-permute-done.19 = bf16[160,4096]{1,0:T(8,128)(2,1)S(1)} collective-permute-done((bf16[160,4096]{1,0:T(8,128)(2,1)S(1)}, bf16[160,4096]{1,0:T(8,128)(2,1)S(1)}, u32[]{:S(2)}, u32[]{:S(2)}) %collective-permute-start.19) | collective-permute-done | bytes 1310752 | tf_op jit(solution)/shard_map/ppermute | solution.py:97
  817.4 14.6 %collective-permute-done.12 = bf16[144,4096]{1,0:T(8,128)(2,1)} collective-permute-done((bf16[144,4096]{1,0:T(8,128)(2,1)S(1)}, bf16[144,4096]{1,0:T(8,128)(2,1)}, u32[]{:S(2)}, u32[]{:S(2)}) %collective-permute-start.12) | collective-permute-done | bytes 1179680 | tf_op jit(solution)/shard_map/ppermute | solution.py:97
  832.0 7.1 collective-permute-done.15
  843.1 24.0 %collective-permute-done.20 = bf16[160,4096]{1,0:T(8,128)(2,1)S(1)} collective-permute-done((bf16[160,4096]{1,0:T(8,128)(2,1)S(1)}, bf16[160,4096]{1,0:T(8,128)(2,1)S(1)}, u32[]{:S(2)}, u32[]{:S(2)}) %collective-permute-start.20) | collective-permute-done | bytes 1310752 | tf_op jit(solution)/shard_map/ppermute | solution.py:97
  (623 shorter events, 207.6 us)
Async XLA Ops:
  6.5 76.7 %all-gather.11.cloned.1.call-start = ((), (), s32[]{:S(2)}) async-start(), calls=%async_computation | async-start | bytes 13369344 | tf_op jit(solution)/shard_map/all_gather | solution.py:54
  8.7 157.2 %all-gather.17.cloned.1.call-start = ((), (), s32[]{:S(2)}) async-start(), calls=%async_computation.3 | async-start | bytes 15597568 | tf_op jit(solution)/shard_map/all_gather | solution.py:54
  11.0 304.1 %all-gather.13.cloned.1.call-start = ((), (), s32[]{:S(2)}) async-start(), calls=%async_computation.1 | async-start | bytes 20054016 | tf_op jit(solution)/shard_map/all_gather | solution.py:54
  13.6 415.9 %all-gather.15.cloned.1.call-start = ((), (), s32[]{:S(2)}) async-start(), calls=%async_computation.2 | async-start | bytes 22282240 | tf_op jit(solution)/shard_map/all_gather | solution.py:54
  150.9 45.7 %collective-permute-start = (bf16[8,96,4096]{2,1,0:T(8,128)(2,1)}, bf16[8,96,4096]{2,1,0:T(8,128)(2,1)}, u32[]{:S(2)}, u32[]{:S(2)}) collective-permute-start(bf16[8,96,4096]{2,1,0:T(8,128)(2,1)} %bitcast.654), channel_id=1, source_target_pairs={{0,1},{1,0},{2,3},{3,2},{4,5},{5,4},{6,7},{7,6},{8,9},{9,8},{10,11... | collective-permute-start | bytes 18874376 | tf_op jit(solution)/shard_map/ppermute | solution.py:80
  198.4 36.7 %collective-permute-start.1 = (bf16[96,4096]{1,0:T(8,128)(2,1)S(1)}, bf16[96,4096]{1,0:T(8,128)(2,1)S(1)}, u32[]{:S(2)}, u32[]{:S(2)}) collective-permute-start(bf16[96,4096]{1,0:T(8,128)(2,1)S(1)} %fusion.199), channel_id=1, source_target_pairs={{0,2},{1,3},{2,4},{3,5},{4,6},{5,7},{6,8},{7,9},{8,10},{9,11},{10,... | collective-permute-start | bytes 2359304 | tf_op jit(solution)/shard_map/ppermute | solution.py:97
  238.4 36.3 %collective-permute-start.2 = (bf16[96,4096]{1,0:T(8,128)(2,1)S(1)}, bf16[96,4096]{1,0:T(8,128)(2,1)S(1)}, u32[]{:S(2)}, u32[]{:S(2)}) collective-permute-start(bf16[96,4096]{1,0:T(8,128)(2,1)S(1)} %get-tuple-element.404), channel_id=1, source_target_pairs={{0,2},{1,3},{2,4},{3,5},{4,6},{5,7},{6,8},{7,9},{8,10},{9,11},{10,... | collective-permute-start | bytes 2359304 | tf_op jit(solution)/shard_map/ppermute | solution.py:97
  240.8 35.4 %collective-permute-start.5 = (bf16[96,4096]{1,0:T(8,128)(2,1)S(1)}, bf16[96,4096]{1,0:T(8,128)(2,1)S(1)}, u32[]{:S(2)}, u32[]{:S(2)}) collective-permute-start(bf16[96,4096]{1,0:T(8,128)(2,1)S(1)} %get-tuple-element.405), channel_id=1, source_target_pairs={{0,14},{1,15},{2,0},{3,1},{4,2},{5,3},{6,4},{7,5},{8,6},{9,7},{10,... | collective-permute-start | bytes 2359304 | tf_op jit(solution)/shard_map/ppermute | solution.py:97
  257.6 306.4 %collective-permute-start.24 = (bf16[8,112,4096]{2,1,0:T(8,128)(2,1)}, bf16[8,112,4096]{2,1,0:T(8,128)(2,1)}, u32[]{:S(2)}, u32[]{:S(2)}) collective-permute-start(bf16[8,112,4096]{2,1,0:T(8,128)(2,1)} %bitcast.178), channel_id=1, source_target_pairs={{0,1},{1,0},{2,3},{3,2},{4,5},{5,4},{6,7},{7,6},{8,9},{9,8},{10,11... | collective-permute-start | bytes 22020104 | tf_op jit(solution)/shard_map/ppermute | solution.py:80
  281.1 253.5 %collective-permute-start.3 = (bf16[96,4096]{1,0:T(8,128)(2,1)}, bf16[96,4096]{1,0:T(8,128)(2,1)}, u32[]{:S(2)}, u32[]{:S(2)}) collective-permute-start(bf16[96,4096]{1,0:T(8,128)(2,1)} %get-tuple-element.402), channel_id=1, source_target_pairs={{0,2},{1,3},{2,4},{3,5},{4,6},{5,7},{6,8},{7,9},{8,10},{9,11},{10,... | collective-permute-start | bytes 2359304 | tf_op jit(solution)/shard_map/ppermute | solution.py:97
  283.9 250.7 %collective-permute-start.6 = (bf16[96,4096]{1,0:T(8,128)(2,1)}, bf16[96,4096]{1,0:T(8,128)(2,1)}, u32[]{:S(2)}, u32[]{:S(2)}) collective-permute-start(bf16[96,4096]{1,0:T(8,128)(2,1)} %get-tuple-element.403), channel_id=1, source_target_pairs={{0,14},{1,15},{2,0},{3,1},{4,2},{5,3},{6,4},{7,5},{8,6},{9,7},{10,... | collective-permute-start | bytes 2359304 | tf_op jit(solution)/shard_map/ppermute | solution.py:97
  413.6 197.3 %collective-permute-start.8 = (bf16[8,144,4096]{2,1,0:T(8,128)(2,1)}, bf16[8,144,4096]{2,1,0:T(8,128)(2,1)}, u32[]{:S(2)}, u32[]{:S(2)}) collective-permute-start(bf16[8,144,4096]{2,1,0:T(8,128)(2,1)} %bitcast.136), channel_id=1, source_target_pairs={{0,1},{1,0},{2,3},{3,2},{4,5},{5,4},{6,7},{7,6},{8,9},{9,8},{10,11... | collective-permute-start | bytes 28311560 | tf_op jit(solution)/shard_map/ppermute | solution.py:80
  534.4 81.5 %collective-permute-start.16 = (bf16[8,160,4096]{2,1,0:T(8,128)(2,1)}, bf16[8,160,4096]{2,1,0:T(8,128)(2,1)S(1)}, u32[]{:S(2)}, u32[]{:S(2)}) collective-permute-start(bf16[8,160,4096]{2,1,0:T(8,128)(2,1)} %bitcast.653), channel_id=1, source_target_pairs={{0,1},{1,0},{2,3},{3,2},{4,5},{5,4},{6,7},{7,6},{8,9},{9,8},{10,11... | collective-permute-start | bytes 31457288 | tf_op jit(solution)/shard_map/ppermute | solution.py:80
  566.9 52.1 %collective-permute-start.25 = (bf16[112,4096]{1,0:T(8,128)(2,1)}, bf16[112,4096]{1,0:T(8,128)(2,1)S(1)}, u32[]{:S(2)}, u32[]{:S(2)}) collective-permute-start(bf16[112,4096]{1,0:T(8,128)(2,1)} %fusion.161), channel_id=1, source_target_pairs={{0,14},{1,15},{2,0},{3,1},{4,2},{5,3},{6,4},{7,5},{8,6},{9,7},{10,... | collective-permute-start | bytes 2752520 | tf_op jit(solution)/shard_map/ppermute | solution.py:97
  623.1 37.6 %collective-permute-start.26 = (bf16[112,4096]{1,0:T(8,128)(2,1)S(1)}, bf16[112,4096]{1,0:T(8,128)(2,1)S(1)}, u32[]{:S(2)}, u32[]{:S(2)}) collective-permute-start(bf16[112,4096]{1,0:T(8,128)(2,1)S(1)} %get-tuple-element.398), channel_id=1, source_target_pairs={{0,14},{1,15},{2,0},{3,1},{4,2},{5,3},{6,4},{7,5},{8,6},{9,7},{10,... | collective-permute-start | bytes 2752520 | tf_op jit(solution)/shard_map/ppermute | solution.py:97
  625.2 42.6 %collective-permute-start.29 = (bf16[112,4096]{1,0:T(8,128)(2,1)S(1)}, bf16[112,4096]{1,0:T(8,128)(2,1)}, u32[]{:S(2)}, u32[]{:S(2)}) collective-permute-start(bf16[112,4096]{1,0:T(8,128)(2,1)S(1)} %get-tuple-element.399), channel_id=1, source_target_pairs={{0,2},{1,3},{2,4},{3,5},{4,6},{5,7},{6,8},{7,9},{8,10},{9,11},{10,... | collective-permute-start | bytes 2752520 | tf_op jit(solution)/shard_map/ppermute | solution.py:97
  645.1 40.8 %collective-permute-start.10 = (bf16[144,4096]{1,0:T(8,128)(2,1)S(1)}, bf16[144,4096]{1,0:T(8,128)(2,1)S(1)}, u32[]{:S(2)}, u32[]{:S(2)}) collective-permute-start(bf16[144,4096]{1,0:T(8,128)(2,1)S(1)} %get-tuple-element.392), channel_id=1, source_target_pairs={{0,14},{1,15},{2,0},{3,1},{4,2},{5,3},{6,4},{7,5},{8,6},{9,7},{10,... | collective-permute-start | bytes 3538952 | tf_op jit(solution)/shard_map/ppermute | solution.py:97
  646.5 46.5 %collective-permute-start.13 = (bf16[144,4096]{1,0:T(8,128)(2,1)S(1)}, bf16[144,4096]{1,0:T(8,128)(2,1)S(1)}, u32[]{:S(2)}, u32[]{:S(2)}) collective-permute-start(bf16[144,4096]{1,0:T(8,128)(2,1)S(1)} %get-tuple-element.393), channel_id=1, source_target_pairs={{0,2},{1,3},{2,4},{3,5},{4,6},{5,7},{6,8},{7,9},{8,10},{9,11},{10,... | collective-permute-start | bytes 3538952 | tf_op jit(solution)/shard_map/ppermute | solution.py:97
  652.2 68.9 %collective-permute-start.18 = (bf16[160,4096]{1,0:T(8,128)(2,1)S(1)}, bf16[160,4096]{1,0:T(8,128)(2,1)S(1)}, u32[]{:S(2)}, u32[]{:S(2)}) collective-permute-start(bf16[160,4096]{1,0:T(8,128)(2,1)S(1)} %get-tuple-element.386), channel_id=1, source_target_pairs={{0,2},{1,3},{2,4},{3,5},{4,6},{5,7},{6,8},{7,9},{8,10},{9,11},{10,... | collective-permute-start | bytes 3932168 | tf_op jit(solution)/shard_map/ppermute | solution.py:97
  660.8 60.5 %collective-permute-start.21 = (bf16[160,4096]{1,0:T(8,128)(2,1)S(1)}, bf16[160,4096]{1,0:T(8,128)(2,1)S(1)}, u32[]{:S(2)}, u32[]{:S(2)}) collective-permute-start(bf16[160,4096]{1,0:T(8,128)(2,1)S(1)} %get-tuple-element.387), channel_id=1, source_target_pairs={{0,14},{1,15},{2,0},{3,1},{4,2},{5,3},{6,4},{7,5},{8,6},{9,7},{10,... | collective-permute-start | bytes 3932168 | tf_op jit(solution)/shard_map/ppermute | solution.py:97
  672.2 61.5 %collective-permute-start.27 = (bf16[112,4096]{1,0:T(8,128)(2,1)S(1)}, bf16[112,4096]{1,0:T(8,128)(2,1)S(1)}, u32[]{:S(2)}, u32[]{:S(2)}) collective-permute-start(bf16[112,4096]{1,0:T(8,128)(2,1)S(1)} %get-tuple-element.396), channel_id=1, source_target_pairs={{0,14},{1,15},{2,0},{3,1},{4,2},{5,3},{6,4},{7,5},{8,6},{9,7},{10,... | collective-permute-start | bytes 2752520 | tf_op jit(solution)/shard_map/ppermute | solution.py:97
  686.0 54.9 %collective-permute-start.30 = (bf16[112,4096]{1,0:T(8,128)(2,1)S(1)}, bf16[112,4096]{1,0:T(8,128)(2,1)}, u32[]{:S(2)}, u32[]{:S(2)}) collective-permute-start(bf16[112,4096]{1,0:T(8,128)(2,1)S(1)} %get-tuple-element.397), channel_id=1, source_target_pairs={{0,2},{1,3},{2,4},{3,5},{4,6},{5,7},{6,8},{7,9},{8,10},{9,11},{10,... | collective-permute-start | bytes 2752520 | tf_op jit(solution)/shard_map/ppermute | solution.py:97
  697.9 61.0 %collective-permute-start.11 = (bf16[144,4096]{1,0:T(8,128)(2,1)S(1)}, bf16[144,4096]{1,0:T(8,128)(2,1)S(1)}, u32[]{:S(2)}, u32[]{:S(2)}) collective-permute-start(bf16[144,4096]{1,0:T(8,128)(2,1)S(1)} %get-tuple-element.390), channel_id=1, source_target_pairs={{0,14},{1,15},{2,0},{3,1},{4,2},{5,3},{6,4},{7,5},{8,6},{9,7},{10,... | collective-permute-start | bytes 3538952 | tf_op jit(solution)/shard_map/ppermute | solution.py:97
  721.2 44.9 %collective-permute-start.14 = (bf16[144,4096]{1,0:T(8,128)(2,1)S(1)}, bf16[144,4096]{1,0:T(8,128)(2,1)S(1)}, u32[]{:S(2)}, u32[]{:S(2)}) collective-permute-start(bf16[144,4096]{1,0:T(8,128)(2,1)S(1)} %get-tuple-element.391), channel_id=1, source_target_pairs={{0,2},{1,3},{2,4},{3,5},{4,6},{5,7},{6,8},{7,9},{8,10},{9,11},{10,... | collective-permute-start | bytes 3538952 | tf_op jit(solution)/shard_map/ppermute | solution.py:97
  725.5 68.7 %collective-permute-start.19 = (bf16[160,4096]{1,0:T(8,128)(2,1)S(1)}, bf16[160,4096]{1,0:T(8,128)(2,1)S(1)}, u32[]{:S(2)}, u32[]{:S(2)}) collective-permute-start(bf16[160,4096]{1,0:T(8,128)(2,1)S(1)} %get-tuple-element.384), channel_id=1, source_target_pairs={{0,2},{1,3},{2,4},{3,5},{4,6},{5,7},{6,8},{7,9},{8,10},{9,11},{10,... | collective-permute-start | bytes 3932168 | tf_op jit(solution)/shard_map/ppermute | solution.py:97
  733.8 60.6 %collective-permute-start.22 = (bf16[160,4096]{1,0:T(8,128)(2,1)S(1)}, bf16[160,4096]{1,0:T(8,128)(2,1)S(1)}, u32[]{:S(2)}, u32[]{:S(2)}) collective-permute-start(bf16[160,4096]{1,0:T(8,128)(2,1)S(1)} %get-tuple-element.385), channel_id=1, source_target_pairs={{0,14},{1,15},{2,0},{3,1},{4,2},{5,3},{6,4},{7,5},{8,6},{9,7},{10,... | collective-permute-start | bytes 3932168 | tf_op jit(solution)/shard_map/ppermute | solution.py:97
  745.9 60.9 %collective-permute-start.28 = (bf16[112,4096]{1,0:T(8,128)(2,1)}, bf16[112,4096]{1,0:T(8,128)(2,1)}, u32[]{:S(2)}, u32[]{:S(2)}) collective-permute-start(bf16[112,4096]{1,0:T(8,128)(2,1)} %get-tuple-element.394), channel_id=1, source_target_pairs={{0,14},{1,15},{2,0},{3,1},{4,2},{5,3},{6,4},{7,5},{8,6},{9,7},{10,... | collective-permute-start | bytes 2752520 | tf_op jit(solution)/shard_map/ppermute | solution.py:97
  759.0 54.9 %collective-permute-start.31 = (bf16[112,4096]{1,0:T(8,128)(2,1)S(1)}, bf16[112,4096]{1,0:T(8,128)(2,1)}, u32[]{:S(2)}, u32[]{:S(2)}) collective-permute-start(bf16[112,4096]{1,0:T(8,128)(2,1)S(1)} %get-tuple-element.395), channel_id=1, source_target_pairs={{0,2},{1,3},{2,4},{3,5},{4,6},{5,7},{6,8},{7,9},{8,10},{9,11},{10,... | collective-permute-start | bytes 2752520 | tf_op jit(solution)/shard_map/ppermute | solution.py:97
  770.9 61.1 %collective-permute-start.12 = (bf16[144,4096]{1,0:T(8,128)(2,1)S(1)}, bf16[144,4096]{1,0:T(8,128)(2,1)}, u32[]{:S(2)}, u32[]{:S(2)}) collective-permute-start(bf16[144,4096]{1,0:T(8,128)(2,1)S(1)} %get-tuple-element.388), channel_id=1, source_target_pairs={{0,14},{1,15},{2,0},{3,1},{4,2},{5,3},{6,4},{7,5},{8,6},{9,7},{10,... | collective-permute-start | bytes 3538952 | tf_op jit(solution)/shard_map/ppermute | solution.py:97
  794.3 44.9 %collective-permute-start.15 = (bf16[144,4096]{1,0:T(8,128)(2,1)S(1)}, bf16[144,4096]{1,0:T(8,128)(2,1)}, u32[]{:S(2)}, u32[]{:S(2)}) collective-permute-start(bf16[144,4096]{1,0:T(8,128)(2,1)S(1)} %get-tuple-element.389), channel_id=1, source_target_pairs={{0,2},{1,3},{2,4},{3,5},{4,6},{5,7},{6,8},{7,9},{8,10},{9,11},{10,... | collective-permute-start | bytes 3538952 | tf_op jit(solution)/shard_map/ppermute | solution.py:97
  798.6 68.5 %collective-permute-start.20 = (bf16[160,4096]{1,0:T(8,128)(2,1)S(1)}, bf16[160,4096]{1,0:T(8,128)(2,1)S(1)}, u32[]{:S(2)}, u32[]{:S(2)}) collective-permute-start(bf16[160,4096]{1,0:T(8,128)(2,1)S(1)} %get-tuple-element.382), channel_id=1, source_target_pairs={{0,2},{1,3},{2,4},{3,5},{4,6},{5,7},{6,8},{7,9},{8,10},{9,11},{10,... | collective-permute-start | bytes 3932168 | tf_op jit(solution)/shard_map/ppermute | solution.py:97
  806.8 60.4 %collective-permute-start.23 = (bf16[160,4096]{1,0:T(8,128)(2,1)S(1)}, bf16[160,4096]{1,0:T(8,128)(2,1)S(1)}, u32[]{:S(2)}, u32[]{:S(2)}) collective-permute-start(bf16[160,4096]{1,0:T(8,128)(2,1)S(1)} %get-tuple-element.383), channel_id=1, source_target_pairs={{0,14},{1,15},{2,0},{3,1},{4,2},{5,3},{6,4},{7,5},{8,6},{9,7},{10,... | collective-permute-start | bytes 3932168 | tf_op jit(solution)/shard_map/ppermute | solution.py:97
  (228 other events, 7497.0 us)
Sparse Core Ops, SparseCore 0:
  9.0 74.2 all-gather.10
  84.9 80.9 all-gather.16
  167.5 147.6 all-gather.12
  316.7 112.7 all-gather.14

commit v2 on v1

--- a/solution.py
+++ b/solution.py
@@ -3,7 +3,7 @@
 from jax import lax
 from jax.sharding import PartitionSpec as P
 
-PARTS = (12, 18, 20, 14)
+PARTS = (7, 8, 9, 4, 4)
 
 
 def weights(masks, g):
@@ -51,7 +51,9 @@
 
         tabs = {1: tables(1), -1: tables(-1)}
         outs = []
-        xs = [lax.all_gather(x[lo:hi], 'ep') for lo, hi in zip(cuts, cuts[1:])]
+        xs = []
+        for k, (lo, hi) in enumerate(zip(cuts, cuts[1:])):
+            xs.append(lax.all_gather(x[lo:hi], 'ep'))
         used = {j: (2, 3) if j == far else (0, 2, 3) if j < far else (1, 2, 3) for j in range(1, nz)}
         used[nz - far + 1] = (2, 3)
         used[0] = (0, 1, 2, 3)
@@ -68,17 +70,20 @@
             n = cuts[k + 1] - cuts[k]
             rows = xs[k].reshape(ep * n, d)
             a = jnp.dot(rows, w1[0], preferred_element_type=jnp.float32)
+            rows, a = lax.optimization_barrier((rows, a))
             b = jnp.dot(rows, w3[0], preferred_element_type=jnp.float32)
             h = (jax.nn.silu(a) * b).astype(jnp.bfloat16).reshape(nz, 2, n, -1)
 
-            def out(core):
+            def out(h, core):
                 part = lax.dynamic_index_in_dim(h, core, 1, keepdims=False).reshape(nz * n, -1)
                 o = jnp.dot(part, w2[0], preferred_element_type=jnp.float32)
                 return o.astype(jnp.bfloat16).reshape(nz, n, d)
 
-            other = out(1 - c)
+            other = out(h, 1 - c)
             par = lax.ppermute(other, 'ep', swap)
-            own = out(c)
+            own = out(lax.optimization_barrier((h, other))[0], c)
+            if k + 1 < len(PARTS):
+                xs[k + 1] = lax.optimization_barrier((xs[k + 1], own))[0]
 
             def at(v, j):
                 return lax.dynamic_index_in_dim(v, (z + j) % nz, 0, keepdims=False)
@@ -102,7 +107,6 @@
             outs.append(merge([long, short, at(own, 0), at(par, 0)], at_place(0, 0, 1, 2, 3)))
         return jnp.concatenate(outs, axis=0)
 
-
     spec = P(('dp', 'ep'), None)
     wspec = P('ep', None, None)
     return jax.shard_map(local, mesh=mesh, in_specs=(spec, spec, spec, wspec, wspec, wspec),

time: 888 us -> 864 us (0.973)
  the two profiles are of different devices: /device:TPU:85 before, /device:TPU:22 now
where the time goes in v2:
time: 864 us; the launch traced here: 854 us
  matrix products  430 us (50%)
  waiting for transfers between devices  216 us (25%)
  other arithmetic  100 us (12%)
  starting transfers between devices  48.2 us (6%)
  blocking collectives  23 us (3%)
  local copies, waits for them, and re-layouts  18.3 us (2%)
  between operations  18.1 us (2%)
    ppermute x35, waiting for transfers between devices, walk(): msg = lax.ppermute(msg, 'ep', perm_z(step))  182 us
    dot_general x10, matrix products, out(): o = jnp.dot(part, w2[0], preferred_element_type=jnp.float32)  155 us
    dot_general x5, matrix products, local(): a = jnp.dot(rows, w1[0], preferred_element_type=jnp.float32)  139 us
    dot_general x5, matrix products, local(): b = jnp.dot(rows, w3[0], preferred_element_type=jnp.float32)  136 us
    convert_element_type x20, other arithmetic, merge(): return total.astype(jnp.bfloat16)  64.3 us
    ppermute x35, starting transfers between devices, walk(): msg = lax.ppermute(msg, 'ep', perm_z(step))  46.9 us
    all_gather x5, waiting for transfers between devices, local(): xs.append(lax.all_gather(x[lo:hi], 'ep'))  33.9 us
    all_gather x1, blocking collectives, local(): lax.all_gather(jnp.concatenate([route_idx.astype(jnp.float32), gates], ax...  23 us
  transfers between devices with their start and end apart: 45, of which 21 were waited for; matrix products, arithmetic and copies ran while one was open for 64% of the time, Pallas kernels for 0%

profile of v2, /device:TPU:22, one launch (start us, length us, event | category | flops | bytes accessed | tf_op | source)
XLA Modules:
  0.0 853.7 jit_solution(157852439181671457)
XLA Ops:
  17.0 23.0 %all-gather.6 = f32[16,4,512]{2,1,0:T(4,128)S(1)} all-gather(f32[1,4,512]{2,1,0:T(4,128)S(1)} %maximum_bitcast_fusion), channel_id=3, replica_groups=mesh['dp'=4,'ep'=16] {'ep'}, dimensions={0}, use_global_device_ids=true | all-gather | bytes 139264 | tf_op jit(solution)/shard_map/all_gather | solution.py:39
  64.9 30.8 %all-gather.13.cloned.1.call-done = bf16[1792,4096]{1,0:T(8,128)(2,1)} async-done(((bf16[112,4096]{1,0:T(8,128)(2,1)}), bf16[1792,4096]{1,0:T(8,128)(2,1)}) %all-gather.13.cloned.1.call-update) | async-done | bytes 14680080 | tf_op jit(solution)/shard_map/all_gather | solution.py:56
  95.6 27.6 %fusion.35 = f32[1792,1536]{1,0:T(8,128)S(1)} fusion(bf16[1792,4096]{1,0:T(8,128)(2,1)} %all-gather.13.cloned.1.call-done, bf16[1,4096,1536]{2,1,0:T(8,128)(2,1)} %param.9), kind=kOutput, calls=%fused_computation.39 | convolution fusion | flops 22548578304 | bytes 38273024 | tf_op jit(solution)/shard_map/dot_general | solution.py:72
  123.5 30.0 %multiply_convert_fusion.1 = bf16[1792,1536]{1,0:T(8,128)(2,1)S(1)} fusion(f32[1792,1536]{1,0:T(8,128)S(1)} %fusion.35, bf16[1792,4096]{1,0:T(8,128)(2,1)} %all-gather.13.cloned.1.call-done, bf16[1,4096,1536]{2,1,0:T(8,128)(2,1)} %param.10), kind=kOutput, calls=%fused_computation.43 | convolution fusion | flops 22565093376 | bytes 43778048 | tf_op jit(solution)/shard_map/dot_general | solution.py:74
  153.7 17.2 %fusion.50 = bf16[896,4096]{1,0:T(8,128)(2,1)} fusion(bf16[896,1536]{1,0:T(8,128)(2,1)S(1)} %bitcast.828, bf16[1,1536,4096]{2,1,0:T(8,128)(2,1)} %param.11), kind=kOutput, calls=%fused_computation.46 | convolution fusion | flops 11277959168 | bytes 22675456 | tf_op jit(solution)/shard_map/dot_general | solution.py:79
  171.4 13.4 %fusion.53 = bf16[896,4096]{1,0:T(8,128)(2,1)} fusion(bf16[896,1536]{1,0:T(8,128)(2,1)S(1)} %bitcast.827, bf16[1,1536,4096]{2,1,0:T(8,128)(2,1)S(1)} %bitcast.883), kind=kOutput, calls=%fused_computation.47 | convolution fusion | flops 11277959168 | bytes 22675456 | tf_op jit(solution)/shard_map/dot_general | solution.py:79
  187.9 34.3 %fusion.33 = f32[2048,1536]{1,0:T(8,128)} fusion(bf16[2048,4096]{1,0:T(8,128)(2,1)} %all-gather.15.cloned.1.call-done, bf16[1,4096,1536]{2,1,0:T(8,128)(2,1)} %param.9), kind=kOutput, calls=%fused_computation.37 | convolution fusion | flops 25769803776 | bytes 41943040 | tf_op jit(solution)/shard_map/dot_general | solution.py:72
  222.2 34.4 %multiply_convert_fusion = bf16[2048,1536]{1,0:T(8,128)(2,1)S(1)} fusion(f32[2048,1536]{1,0:T(8,128)} %fusion.33, bf16[2048,4096]{1,0:T(8,128)(2,1)} %all-gather.15.cloned.1.call-done, bf16[1,4096,1536]{2,1,0:T(8,128)(2,1)} %param.10), kind=kOutput, calls=%fused_computation.41 | convolution fusion | flops 25788678144 | bytes 48234496 | tf_op jit(solution)/shard_map/dot_general | solution.py:74
  256.9 28.9 %fusion.44 = bf16[1024,4096]{1,0:T(8,128)(2,1)} fusion(bf16[1024,1536]{1,0:T(8,128)(2,1)S(1)} %bitcast.822, bf16[1,1536,4096]{2,1,0:T(8,128)(2,1)S(1)} %bitcast.885), kind=kOutput, calls=%fused_computation.44 | convolution fusion | flops 12889096192 | bytes 24117248 | tf_op jit(solution)/shard_map/dot_general | solution.py:79
  286.2 15.2 %fusion.47 = bf16[1024,4096]{1,0:T(8,128)(2,1)} fusion(bf16[1024,1536]{1,0:T(8,128)(2,1)S(1)} %bitcast.821, bf16[1,1536,4096]{2,1,0:T(8,128)(2,1)S(1)} %bitcast.885), kind=kOutput, calls=%fused_computation.45 | convolution fusion | flops 12889096192 | bytes 24117248 | tf_op jit(solution)/shard_map/dot_general | solution.py:79
  304.6 38.0 %fusion.31 = f32[2304,1536]{1,0:T(8,128)} fusion(bf16[2304,4096]{1,0:T(8,128)(2,1)} %all-gather.17.cloned.1.call-done, bf16[1,4096,1536]{2,1,0:T(8,128)(2,1)} %param.9), kind=kOutput, calls=%fused_computation.35 | convolution fusion | flops 28991029248 | bytes 45613056 | tf_op jit(solution)/shard_map/dot_general | solution.py:72
  342.5 37.6 %fusion.37 = bf16[2304,1536]{1,0:T(8,128)(2,1)S(1)} fusion(bf16[2304,4096]{1,0:T(8,128)(2,1)} %all-gather.17.cloned.1.call-done, bf16[1,4096,1536]{2,1,0:T(8,128)(2,1)} %param.10, f32[2304,1536]{1,0:T(8,128)} %fusion.31), kind=kOutput, calls=%fused_computation.42 | convolution fusion | flops 29012262912 | bytes 52690944 | tf_op jit(solution)/shard_map/dot_general | solution.py:74
  380.5 20.1 %convolution_convert_fusion.1 = bf16[1152,4096]{1,0:T(8,128)(2,1)} fusion(bf16[1152,1536]{1,0:T(8,128)(2,1)S(1)} %bitcast.820, bf16[1,1536,4096]{2,1,0:T(8,128)(2,1)} %param.11), kind=kOutput, calls=%fused_computation.3 | convolution fusion | flops 14500233216 | bytes 25559040 | tf_op jit(solution)/shard_map/dot_general | solution.py:79
  401.2 20.5 %convolution_convert_fusion = bf16[1152,4096]{1,0:T(8,128)(2,1)} fusion(bf16[1152,1536]{1,0:T(8,128)(2,1)S(1)} %bitcast.819, bf16[1,1536,4096]{2,1,0:T(8,128)(2,1)} %param.11), kind=kOutput, calls=%fused_computation.2 | convolution fusion | flops 14500233216 | bytes 25559040 | tf_op jit(solution)/shard_map/dot_general | solution.py:79
  421.7 19.6 %fusion.29 = f32[1024,1536]{1,0:T(8,128)} fusion(bf16[1024,4096]{1,0:T(8,128)(2,1)} %all-gather.19.cloned.1.call-done, bf16[1,4096,1536]{2,1,0:T(8,128)(2,1)} %param.9), kind=kOutput, calls=%fused_computation.33 | convolution fusion | flops 12884901888 | bytes 27262976 | tf_op jit(solution)/shard_map/dot_general | solution.py:72
  441.3 17.3 %multiply_convert_fusion.3 = bf16[1024,1536]{1,0:T(8,128)(2,1)S(1)} fusion(f32[1024,1536]{1,0:T(8,128)} %fusion.29, bf16[1024,4096]{1,0:T(8,128)(2,1)S(1)} %copy-done.257, bf16[1,4096,1536]{2,1,0:T(8,128)(2,1)} %param.10), kind=kOutput, calls=%fused_computation.49 | convolution fusion | flops 12894339072 | bytes 30408704 | tf_op jit(solution)/shard_map/dot_general | solution.py:74
  458.8 8.6 %fusion.56 = bf16[512,4096]{1,0:T(8,128)(2,1)} fusion(bf16[512,1536]{1,0:T(8,128)(2,1)S(1)} %bitcast.832, bf16[1,1536,4096]{2,1,0:T(8,128)(2,1)S(1)} %bitcast.887), kind=kOutput, calls=%fused_computation.50 | convolution fusion | flops 6444548096 | bytes 18350080 | tf_op jit(solution)/shard_map/dot_general | solution.py:79
  467.7 8.4 fusion.59
  484.3 19.7 %fusion.27 = f32[1024,1536]{1,0:T(8,128)} fusion(bf16[1024,4096]{1,0:T(8,128)(2,1)} %all-gather.21.cloned.1.call-done, bf16[1,4096,1536]{2,1,0:T(8,128)(2,1)} %param.9), kind=kOutput, calls=%fused_computation.31 | convolution fusion | flops 12884901888 | bytes 27262976 | tf_op jit(solution)/shard_map/dot_general | solution.py:72
  512.7 16.7 %multiply_convert_fusion.2 = bf16[1024,1536]{1,0:T(8,128)(2,1)S(1)} fusion(f32[1024,1536]{1,0:T(8,128)} %fusion.27, bf16[1024,4096]{1,0:T(8,128)(2,1)} %all-gather.21.cloned.1.call-done, bf16[1,4096,1536]{2,1,0:T(8,128)(2,1)S(1)} %bitcast.881), kind=kOutput, calls=%fused_computation.48 | convolution fusion | flops 12894339072 | bytes 30408704 | tf_op jit(solution)/shard_map/dot_general | solution.py:74
  539.9 12.8 %fusion.62 = bf16[512,4096]{1,0:T(8,128)(2,1)} fusion(bf16[512,1536]{1,0:T(8,128)(2,1)S(1)} %bitcast.829, bf16[1,1536,4096]{2,1,0:T(8,128)(2,1)} %param.11), kind=kOutput, calls=%fused_computation.52 | convolution fusion | flops 6444548096 | bytes 18350080 | tf_op jit(solution)/shard_map/dot_general | solution.py:79
  559.6 9.8 %fusion.65 = bf16[512,4096]{1,0:T(8,128)(2,1)S(1)} fusion(bf16[512,1536]{1,0:T(8,128)(2,1)S(1)} %bitcast.830, bf16[1,1536,4096]{2,1,0:T(8,128)(2,1)} %param.11), kind=kOutput, calls=%fused_computation.53 | convolution fusion | flops 6444548096 | bytes 18350080 | tf_op jit(solution)/shard_map/dot_general | solution.py:79
  569.5 10.3 %collective-permute-done.4 = bf16[112,4096]{1,0:T(8,128)(2,1)S(1)} collective-permute-done((bf16[112,4096]{1,0:T(8,128)(2,1)S(1)}, bf16[112,4096]{1,0:T(8,128)(2,1)S(1)}, u32[]{:S(2)}, u32[]{:S(2)}) %collective-permute-start.4) | collective-permute-done | bytes 917536 | tf_op jit(solution)/shard_map/ppermute | solution.py:102
  613.8 19.9 %collective-permute-done.26 = bf16[64,4096]{1,0:T(8,128)(2,1)S(1)} collective-permute-done((bf16[64,4096]{1,0:T(8,128)(2,1)S(1)}, bf16[64,4096]{1,0:T(8,128)(2,1)S(1)}, u32[]{:S(2)}, u32[]{:S(2)}) %collective-permute-start.26) | collective-permute-done | bytes 524320 | tf_op jit(solution)/shard_map/ppermute | solution.py:102
  645.3 14.5 %collective-permute-done.17 = bf16[144,4096]{1,0:T(8,128)(2,1)S(1)} collective-permute-done((bf16[144,4096]{1,0:T(8,128)(2,1)S(1)}, bf16[144,4096]{1,0:T(8,128)(2,1)S(1)}, u32[]{:S(2)}, u32[]{:S(2)}) %collective-permute-start.17) | collective-permute-done | bytes 1179680 | tf_op jit(solution)/shard_map/ppermute | solution.py:102
  678.7 8.6 %collective-permute-done.13 = bf16[128,4096]{1,0:T(8,128)(2,1)S(1)} collective-permute-done((bf16[128,4096]{1,0:T(8,128)(2,1)S(1)}, bf16[128,4096]{1,0:T(8,128)(2,1)S(1)}, u32[]{:S(2)}, u32[]{:S(2)}) %collective-permute-start.13) | collective-permute-done | bytes 1048608 | tf_op jit(solution)/shard_map/ppermute | solution.py:102
  691.7 20.8 %collective-permute-done.18 = bf16[144,4096]{1,0:T(8,128)(2,1)S(1)} collective-permute-done((bf16[144,4096]{1,0:T(8,128)(2,1)S(1)}, bf16[144,4096]{1,0:T(8,128)(2,1)S(1)}, u32[]{:S(2)}, u32[]{:S(2)}) %collective-permute-start.18) | collective-permute-done | bytes 1179680 | tf_op jit(solution)/shard_map/ppermute | solution.py:102
  728.3 10.3 %collective-permute-done.11 = bf16[128,4096]{1,0:T(8,128)(2,1)S(1)} collective-permute-done((bf16[128,4096]{1,0:T(8,128)(2,1)S(1)}, bf16[128,4096]{1,0:T(8,128)(2,1)S(1)}, u32[]{:S(2)}, u32[]{:S(2)}) %collective-permute-start.11) | collective-permute-done | bytes 1048608 | tf_op jit(solution)/shard_map/ppermute | solution.py:102
  741.3 16.2 %collective-permute-done.14 = bf16[128,4096]{1,0:T(8,128)(2,1)S(1)} collective-permute-done((bf16[128,4096]{1,0:T(8,128)(2,1)S(1)}, bf16[128,4096]{1,0:T(8,128)(2,1)S(1)}, u32[]{:S(2)}, u32[]{:S(2)}) %collective-permute-start.14) | collective-permute-done | bytes 1048608 | tf_op jit(solution)/shard_map/ppermute | solution.py:102
  762.0 20.8 %collective-permute-done.19 = bf16[144,4096]{1,0:T(8,128)(2,1)S(1)} collective-permute-done((bf16[144,4096]{1,0:T(8,128)(2,1)S(1)}, bf16[144,4096]{1,0:T(8,128)(2,1)S(1)}, u32[]{:S(2)}, u32[]{:S(2)}) %collective-permute-start.19) | collective-permute-done | bytes 1179680 | tf_op jit(solution)/shard_map/ppermute | solution.py:102
  796.1 20.3 %collective-permute-done.15 = bf16[128,4096]{1,0:T(8,128)(2,1)S(1)} collective-permute-done((bf16[128,4096]{1,0:T(8,128)(2,1)S(1)}, bf16[128,4096]{1,0:T(8,128)(2,1)S(1)}, u32[]{:S(2)}, u32[]{:S(2)}) %collective-permute-start.15) | collective-permute-done | bytes 1048608 | tf_op jit(solution)/shard_map/ppermute | solution.py:102
  825.7 11.2 %collective-permute-done.20 = bf16[144,4096]{1,0:T(8,128)(2,1)S(1)} collective-permute-done((bf16[144,4096]{1,0:T(8,128)(2,1)S(1)}, bf16[144,4096]{1,0:T(8,128)(2,1)S(1)}, u32[]{:S(2)}, u32[]{:S(2)}) %collective-permute-start.20) | collective-permute-done | bytes 1179680 | tf_op jit(solution)/shard_map/ppermute | solution.py:102
  (750 shorter events, 198.8 us)
Async XLA Ops:
  6.5 89.1 %all-gather.13.cloned.1.call-start = ((), (), s32[]{:S(2)}) async-start(), calls=%async_computation | async-start | bytes 15597568 | tf_op jit(solution)/shard_map/all_gather | solution.py:56
  8.8 179.1 %all-gather.15.cloned.1.call-start = ((), (), s32[]{:S(2)}) async-start(), calls=%async_computation.1 | async-start | bytes 17825792 | tf_op jit(solution)/shard_map/all_gather | solution.py:56
  11.2 293.4 %all-gather.17.cloned.1.call-start = ((), (), s32[]{:S(2)}) async-start(), calls=%async_computation.2 | async-start | bytes 20054016 | tf_op jit(solution)/shard_map/all_gather | solution.py:56
  13.7 407.9 %all-gather.19.cloned.1.call-start = ((), (), s32[]{:S(2)}) async-start(), calls=%async_computation.3 | async-start | bytes 8912896 | tf_op jit(solution)/shard_map/all_gather | solution.py:56
  16.1 460.0 %all-gather.21.cloned.1.call-start = ((), (), s32[]{:S(2)}) async-start(), calls=%async_computation.4 | async-start | bytes 8912896 | tf_op jit(solution)/shard_map/all_gather | solution.py:56
  170.9 130.5 %collective-permute-start = (bf16[8,112,4096]{2,1,0:T(8,128)(2,1)}, bf16[8,112,4096]{2,1,0:T(8,128)(2,1)}, u32[]{:S(2)}, u32[]{:S(2)}) collective-permute-start(bf16[8,112,4096]{2,1,0:T(8,128)(2,1)} %bitcast.890), channel_id=1, source_target_pairs={{0,1},{1,0},{2,3},{3,2},{4,5},{5,4},{6,7},{7,6},{8,9},{9,8},{10,11... | collective-permute-start | bytes 22020104 | tf_op jit(solution)/shard_map/ppermute | solution.py:83
  285.8 303.1 %collective-permute-start.8 = (bf16[8,128,4096]{2,1,0:T(8,128)(2,1)}, bf16[8,128,4096]{2,1,0:T(8,128)(2,1)}, u32[]{:S(2)}, u32[]{:S(2)}) collective-permute-start(bf16[8,128,4096]{2,1,0:T(8,128)(2,1)} %bitcast.889), channel_id=1, source_target_pairs={{0,1},{1,0},{2,3},{3,2},{4,5},{5,4},{6,7},{7,6},{8,9},{9,8},{10,11... | collective-permute-start | bytes 25165832 | tf_op jit(solution)/shard_map/ppermute | solution.py:83
  304.6 171.6 %collective-permute-start.1 = (bf16[112,4096]{1,0:T(8,128)(2,1)}, bf16[112,4096]{1,0:T(8,128)(2,1)}, u32[]{:S(2)}, u32[]{:S(2)}) collective-permute-start(bf16[112,4096]{1,0:T(8,128)(2,1)} %fusion.184), channel_id=1, source_target_pairs={{0,2},{1,3},{2,4},{3,5},{4,6},{5,7},{6,8},{7,9},{8,10},{9,11},{10,... | collective-permute-start | bytes 2752520 | tf_op jit(solution)/shard_map/ppermute | solution.py:102
  400.6 207.5 %collective-permute-start.16 = (bf16[8,144,4096]{2,1,0:T(8,128)(2,1)}, bf16[8,144,4096]{2,1,0:T(8,128)(2,1)}, u32[]{:S(2)}, u32[]{:S(2)}) collective-permute-start(bf16[8,144,4096]{2,1,0:T(8,128)(2,1)} %bitcast.888), channel_id=1, source_target_pairs={{0,1},{1,0},{2,3},{3,2},{4,5},{5,4},{6,7},{7,6},{8,9},{9,8},{10,11... | collective-permute-start | bytes 28311560 | tf_op jit(solution)/shard_map/ppermute | solution.py:83
  467.4 116.3 %collective-permute-start.24 = (bf16[8,64,4096]{2,1,0:T(8,128)(2,1)}, bf16[8,64,4096]{2,1,0:T(8,128)(2,1)}, u32[]{:S(2)}, u32[]{:S(2)}) collective-permute-start(bf16[8,64,4096]{2,1,0:T(8,128)(2,1)} %bitcast.204), channel_id=1, source_target_pairs={{0,1},{1,0},{2,3},{3,2},{4,5},{5,4},{6,7},{7,6},{8,9},{9,8},{10,11... | collective-permute-start | bytes 12582920 | tf_op jit(solution)/shard_map/ppermute | solution.py:83
  552.7 34.3 %collective-permute-start.32 = (bf16[8,64,4096]{2,1,0:T(8,128)(2,1)}, bf16[8,64,4096]{2,1,0:T(8,128)(2,1)}, u32[]{:S(2)}, u32[]{:S(2)}) collective-permute-start(bf16[8,64,4096]{2,1,0:T(8,128)(2,1)} %bitcast.227), channel_id=1, source_target_pairs={{0,1},{1,0},{2,3},{3,2},{4,5},{5,4},{6,7},{7,6},{8,9},{9,8},{10,11... | collective-permute-start | bytes 12582920 | tf_op jit(solution)/shard_map/ppermute | solution.py:83
  591.3 48.8 %collective-permute-start.9 = (bf16[128,4096]{1,0:T(8,128)(2,1)S(1)}, bf16[128,4096]{1,0:T(8,128)(2,1)S(1)}, u32[]{:S(2)}, u32[]{:S(2)}) collective-permute-start(bf16[128,4096]{1,0:T(8,128)(2,1)S(1)} %fusion.146), channel_id=1, source_target_pairs={{0,14},{1,15},{2,0},{3,1},{4,2},{5,3},{6,4},{7,5},{8,6},{9,7},{10,... | collective-permute-start | bytes 3145736 | tf_op jit(solution)/shard_map/ppermute | solution.py:102
  602.6 31.1 %collective-permute-start.26 = (bf16[64,4096]{1,0:T(8,128)(2,1)S(1)}, bf16[64,4096]{1,0:T(8,128)(2,1)S(1)}, u32[]{:S(2)}, u32[]{:S(2)}) collective-permute-start(bf16[64,4096]{1,0:T(8,128)(2,1)S(1)} %get-tuple-element.540), channel_id=1, source_target_pairs={{0,14},{1,15},{2,0},{3,1},{4,2},{5,3},{6,4},{7,5},{8,6},{9,7},{10,... | collective-permute-start | bytes 1572872 | tf_op jit(solution)/shard_map/ppermute | solution.py:102
  605.4 28.6 %collective-permute-start.29 = (bf16[64,4096]{1,0:T(8,128)(2,1)S(1)}, bf16[64,4096]{1,0:T(8,128)(2,1)S(1)}, u32[]{:S(2)}, u32[]{:S(2)}) collective-permute-start(bf16[64,4096]{1,0:T(8,128)(2,1)S(1)} %get-tuple-element.541), channel_id=1, source_target_pairs={{0,2},{1,3},{2,4},{3,5},{4,6},{5,7},{6,8},{7,9},{8,10},{9,11},{10,... | collective-permute-start | bytes 1572872 | tf_op jit(solution)/shard_map/ppermute | solution.py:102
  607.9 56.4 %collective-permute-start.34 = (bf16[64,4096]{1,0:T(8,128)(2,1)S(1)}, bf16[64,4096]{1,0:T(8,128)(2,1)S(1)}, u32[]{:S(2)}, u32[]{:S(2)}) collective-permute-start(bf16[64,4096]{1,0:T(8,128)(2,1)S(1)} %get-tuple-element.534), channel_id=1, source_target_pairs={{0,2},{1,3},{2,4},{3,5},{4,6},{5,7},{6,8},{7,9},{8,10},{9,11},{10,... | collective-permute-start | bytes 1572872 | tf_op jit(solution)/shard_map/ppermute | solution.py:102
  608.0 58.7 %collective-permute-start.37 = (bf16[64,4096]{1,0:T(8,128)(2,1)S(1)}, bf16[64,4096]{1,0:T(8,128)(2,1)S(1)}, u32[]{:S(2)}, u32[]{:S(2)}) collective-permute-start(bf16[64,4096]{1,0:T(8,128)(2,1)S(1)} %get-tuple-element.535), channel_id=1, source_target_pairs={{0,14},{1,15},{2,0},{3,1},{4,2},{5,3},{6,4},{7,5},{8,6},{9,7},{10,... | collective-permute-start | bytes 1572872 | tf_op jit(solution)/shard_map/ppermute | solution.py:102
  636.9 83.0 %collective-permute-start.27 = (bf16[64,4096]{1,0:T(8,128)(2,1)S(1)}, bf16[64,4096]{1,0:T(8,128)(2,1)S(1)}, u32[]{:S(2)}, u32[]{:S(2)}) collective-permute-start(bf16[64,4096]{1,0:T(8,128)(2,1)S(1)} %get-tuple-element.538), channel_id=1, source_target_pairs={{0,14},{1,15},{2,0},{3,1},{4,2},{5,3},{6,4},{7,5},{8,6},{9,7},{10,... | collective-permute-start | bytes 1572872 | tf_op jit(solution)/shard_map/ppermute | solution.py:102
  643.8 34.9 %collective-permute-start.10 = (bf16[128,4096]{1,0:T(8,128)(2,1)S(1)}, bf16[128,4096]{1,0:T(8,128)(2,1)S(1)}, u32[]{:S(2)}, u32[]{:S(2)}) collective-permute-start(bf16[128,4096]{1,0:T(8,128)(2,1)S(1)} %get-tuple-element.522), channel_id=1, source_target_pairs={{0,14},{1,15},{2,0},{3,1},{4,2},{5,3},{6,4},{7,5},{8,6},{9,7},{10,... | collective-permute-start | bytes 3145736 | tf_op jit(solution)/shard_map/ppermute | solution.py:102
  659.9 27.3 %collective-permute-start.13 = (bf16[128,4096]{1,0:T(8,128)(2,1)S(1)}, bf16[128,4096]{1,0:T(8,128)(2,1)S(1)}, u32[]{:S(2)}, u32[]{:S(2)}) collective-permute-start(bf16[128,4096]{1,0:T(8,128)(2,1)S(1)} %get-tuple-element.523), channel_id=1, source_target_pairs={{0,2},{1,3},{2,4},{3,5},{4,6},{5,7},{6,8},{7,9},{8,10},{9,11},{10,... | collective-permute-start | bytes 3145736 | tf_op jit(solution)/shard_map/ppermute | solution.py:102
  664.3 48.2 %collective-permute-start.18 = (bf16[144,4096]{1,0:T(8,128)(2,1)S(1)}, bf16[144,4096]{1,0:T(8,128)(2,1)S(1)}, u32[]{:S(2)}, u32[]{:S(2)}) collective-permute-start(bf16[144,4096]{1,0:T(8,128)(2,1)S(1)} %get-tuple-element.516), channel_id=1, source_target_pairs={{0,2},{1,3},{2,4},{3,5},{4,6},{5,7},{6,8},{7,9},{8,10},{9,11},{10,... | collective-permute-start | bytes 3538952 | tf_op jit(solution)/shard_map/ppermute | solution.py:102
  666.7 47.3 %collective-permute-start.21 = (bf16[144,4096]{1,0:T(8,128)(2,1)S(1)}, bf16[144,4096]{1,0:T(8,128)(2,1)S(1)}, u32[]{:S(2)}, u32[]{:S(2)}) collective-permute-start(bf16[144,4096]{1,0:T(8,128)(2,1)S(1)} %get-tuple-element.517), channel_id=1, source_target_pairs={{0,14},{1,15},{2,0},{3,1},{4,2},{5,3},{6,4},{7,5},{8,6},{9,7},{10,... | collective-permute-start | bytes 3538952 | tf_op jit(solution)/shard_map/ppermute | solution.py:102
  678.7 45.1 %collective-permute-start.30 = (bf16[64,4096]{1,0:T(8,128)(2,1)S(1)}, bf16[64,4096]{1,0:T(8,128)(2,1)S(1)}, u32[]{:S(2)}, u32[]{:S(2)}) collective-permute-start(bf16[64,4096]{1,0:T(8,128)(2,1)S(1)} %get-tuple-element.539), channel_id=1, source_target_pairs={{0,2},{1,3},{2,4},{3,5},{4,6},{5,7},{6,8},{7,9},{8,10},{9,11},{10,... | collective-permute-start | bytes 1572872 | tf_op jit(solution)/shard_map/ppermute | solution.py:102
  687.4 103.9 %collective-permute-start.35 = (bf16[64,4096]{1,0:T(8,128)(2,1)S(1)}, bf16[64,4096]{1,0:T(8,128)(2,1)S(1)}, u32[]{:S(2)}, u32[]{:S(2)}) collective-permute-start(bf16[64,4096]{1,0:T(8,128)(2,1)S(1)} %get-tuple-element.532), channel_id=1, source_target_pairs={{0,2},{1,3},{2,4},{3,5},{4,6},{5,7},{6,8},{7,9},{8,10},{9,11},{10,... | collective-permute-start | bytes 1572872 | tf_op jit(solution)/shard_map/ppermute | solution.py:102
  714.1 43.4 %collective-permute-start.14 = (bf16[128,4096]{1,0:T(8,128)(2,1)S(1)}, bf16[128,4096]{1,0:T(8,128)(2,1)S(1)}, u32[]{:S(2)}, u32[]{:S(2)}) collective-permute-start(bf16[128,4096]{1,0:T(8,128)(2,1)S(1)} %get-tuple-element.521), channel_id=1, source_target_pairs={{0,2},{1,3},{2,4},{3,5},{4,6},{5,7},{6,8},{7,9},{8,10},{9,11},{10,... | collective-permute-start | bytes 3145736 | tf_op jit(solution)/shard_map/ppermute | solution.py:102
  719.8 62.9 %collective-permute-start.19 = (bf16[144,4096]{1,0:T(8,128)(2,1)S(1)}, bf16[144,4096]{1,0:T(8,128)(2,1)S(1)}, u32[]{:S(2)}, u32[]{:S(2)}) collective-permute-start(bf16[144,4096]{1,0:T(8,128)(2,1)S(1)} %get-tuple-element.514), channel_id=1, source_target_pairs={{0,2},{1,3},{2,4},{3,5},{4,6},{5,7},{6,8},{7,9},{8,10},{9,11},{10,... | collective-permute-start | bytes 3538952 | tf_op jit(solution)/shard_map/ppermute | solution.py:102
  723.8 59.0 %collective-permute-start.22 = (bf16[144,4096]{1,0:T(8,128)(2,1)S(1)}, bf16[144,4096]{1,0:T(8,128)(2,1)S(1)}, u32[]{:S(2)}, u32[]{:S(2)}) collective-permute-start(bf16[144,4096]{1,0:T(8,128)(2,1)S(1)} %get-tuple-element.515), channel_id=1, source_target_pairs={{0,14},{1,15},{2,0},{3,1},{4,2},{5,3},{6,4},{7,5},{8,6},{9,7},{10,... | collective-permute-start | bytes 3538952 | tf_op jit(solution)/shard_map/ppermute | solution.py:102
  738.6 53.0 %collective-permute-start.38 = (bf16[64,4096]{1,0:T(8,128)(2,1)S(1)}, bf16[64,4096]{1,0:T(8,128)(2,1)S(1)}, u32[]{:S(2)}, u32[]{:S(2)}) collective-permute-start(bf16[64,4096]{1,0:T(8,128)(2,1)S(1)} %get-tuple-element.533), channel_id=1, source_target_pairs={{0,14},{1,15},{2,0},{3,1},{4,2},{5,3},{6,4},{7,5},{8,6},{9,7},{10,... | collective-permute-start | bytes 1572872 | tf_op jit(solution)/shard_map/ppermute | solution.py:102
  757.6 83.8 %collective-permute-start.31 = (bf16[64,4096]{1,0:T(8,128)(2,1)S(1)}, bf16[64,4096]{1,0:T(8,128)(2,1)S(1)}, u32[]{:S(2)}, u32[]{:S(2)}) collective-permute-start(bf16[64,4096]{1,0:T(8,128)(2,1)S(1)} %get-tuple-element.537), channel_id=1, source_target_pairs={{0,2},{1,3},{2,4},{3,5},{4,6},{5,7},{6,8},{7,9},{8,10},{9,11},{10,... | collective-permute-start | bytes 1572872 | tf_op jit(solution)/shard_map/ppermute | solution.py:102
  782.8 33.7 %collective-permute-start.15 = (bf16[128,4096]{1,0:T(8,128)(2,1)S(1)}, bf16[128,4096]{1,0:T(8,128)(2,1)S(1)}, u32[]{:S(2)}, u32[]{:S(2)}) collective-permute-start(bf16[128,4096]{1,0:T(8,128)(2,1)S(1)} %get-tuple-element.519), channel_id=1, source_target_pairs={{0,2},{1,3},{2,4},{3,5},{4,6},{5,7},{6,8},{7,9},{8,10},{9,11},{10,... | collective-permute-start | bytes 3145736 | tf_op jit(solution)/shard_map/ppermute | solution.py:102
  782.9 35.0 %collective-permute-start.12 = (bf16[128,4096]{1,0:T(8,128)(2,1)S(1)}, bf16[128,4096]{1,0:T(8,128)(2,1)S(1)}, u32[]{:S(2)}, u32[]{:S(2)}) collective-permute-start(bf16[128,4096]{1,0:T(8,128)(2,1)S(1)} %get-tuple-element.518), channel_id=1, source_target_pairs={{0,14},{1,15},{2,0},{3,1},{4,2},{5,3},{6,4},{7,5},{8,6},{9,7},{10,... | collective-permute-start | bytes 3145736 | tf_op jit(solution)/shard_map/ppermute | solution.py:102
  791.2 33.0 %collective-permute-start.23 = (bf16[144,4096]{1,0:T(8,128)(2,1)S(1)}, bf16[144,4096]{1,0:T(8,128)(2,1)S(1)}, u32[]{:S(2)}, u32[]{:S(2)}) collective-permute-start(bf16[144,4096]{1,0:T(8,128)(2,1)S(1)} %get-tuple-element.513), channel_id=1, source_target_pairs={{0,14},{1,15},{2,0},{3,1},{4,2},{5,3},{6,4},{7,5},{8,6},{9,7},{10,... | collective-permute-start | bytes 3538952 | tf_op jit(solution)/shard_map/ppermute | solution.py:102
  791.6 45.4 %collective-permute-start.20 = (bf16[144,4096]{1,0:T(8,128)(2,1)S(1)}, bf16[144,4096]{1,0:T(8,128)(2,1)S(1)}, u32[]{:S(2)}, u32[]{:S(2)}) collective-permute-start(bf16[144,4096]{1,0:T(8,128)(2,1)S(1)} %get-tuple-element.512), channel_id=1, source_target_pairs={{0,2},{1,3},{2,4},{3,5},{4,6},{5,7},{6,8},{7,9},{8,10},{9,11},{10,... | collective-permute-start | bytes 3538952 | tf_op jit(solution)/shard_map/ppermute | solution.py:102
  (290 other events, 6901.1 us)
Sparse Core Ops, SparseCore 0:
  9.0 86.6 all-gather.12
  97.3 90.6 all-gather.14
  189.6 100.9 all-gather.16
  292.0 70.8 all-gather.18
  364.4 51.3 all-gather.20
